TPU v7x, 32 devices: a whole 2x2x4 slice. The times are simulated.
32 devices in a mesh: grp: 4 (over y, x), row: 8 (over z, core).
Axes of the slice: x: 2, y: 2, z: 4, core: 2. Of those that a mesh axis runs over, the one named last changes fastest.
Arguments:
- a_tiles: bfloat16 [64, 4, 7, 128, 128], P('row', 'grp'), may hold values from -0.5 to 0.5
- a_cols: int32 [64, 4, 7], P('row', 'grp'), may hold values from 0 to 63, as said below
- p_tiles: bfloat16 [64, 4, 128, 128], P('row'), may hold values from -0.5 to 0.5
- p_cols: int32 [64, 4], replicated, may hold values from 0 to 31, as said below
- c_cols: int32 [32, 16], replicated, may hold values from 0 to 31, as said below
Outputs:
- coarse: float32 [32, 16, 128, 128], P('row', 'grp')
Inputs may be any that keep to these rules, and one draw needn't show every extreme that they name: For fine tile row i in block b = i // 8, every entry of a_cols[i] lies in [max(b - 2, 0) * 8, min(b + 3, 8) * 8). For fine tile row i in block b = i // 8, the entries of p_cols[i] are distinct and lie in [(b - 1) * 4, (b + 2) * 4). For coarse tile row c in block t = c // 4, the entries of c_cols[c] are distinct and lie among the 20 coarse tile rows that start at min(max(t - 2, 0), 3) * 4.
All inputs are finite; a program needn't handle non-finite values.
Results may differ from a plain program's by a relative error of at most 0.0003.
Values may be sent and summed in bfloat16 or wider, within the bound.
A program may use at most 128 MiB of HBM per device.

v0:
```python
import jax
import jax.numpy as jnp
from jax import lax
from jax.sharding import PartitionSpec as P

RATIO = 2


highest = lax.Precision.HIGHEST


def passed_along(x, axis, by):
    size = lax.axis_size(axis)
    pairs = [(i, i + by) for i in range(size) if 0 <= i + by < size]
    return lax.ppermute(x, axis, pairs)


def body(a_tiles, a_cols, p_tiles, p_cols, c_cols):
    fine_rows = a_tiles.shape[0]
    coarse_rows = fine_rows // RATIO
    tile_size = a_tiles.shape[-1]
    position = lax.axis_index("row")
    first_row = position * fine_rows
    fetched_rows = []
    for offset in (2, 1, -1, -2):
        fetched_rows.append(passed_along(p_tiles, "row", offset))
    band_tiles = jnp.concatenate(
        [fetched_rows[0], fetched_rows[1], p_tiles, fetched_rows[2], fetched_rows[3]], axis=0
    )
    padded = jnp.pad(p_cols, ((2 * fine_rows, 2 * fine_rows), (0, 0)), constant_values=-1)
    band_cols = lax.dynamic_slice_in_dim(padded, first_row, 5 * fine_rows, 0)
    own_cols = lax.dynamic_slice_in_dim(p_cols, first_row, fine_rows, 0)
    window = (position - 3) * coarse_rows + jnp.arange(7 * coarse_rows, dtype=jnp.int32)
    base_coarse = (position - 1) * coarse_rows
    local_cols = a_cols[:, 0, :] - (first_row - 2 * fine_rows)

    def fine_row(total, inputs):
        a_row, local_row, own_tiles, own_row_cols = inputs
        fetched = band_tiles[local_row]
        fetched_cols = band_cols[local_row]
        products = jnp.einsum("sxy,spyz->spxz", a_row, fetched, preferred_element_type=jnp.float32)
        placing = (fetched_cols[:, :, None] == window[None, None, :]).astype(jnp.float32)
        spread = jnp.einsum("spxz,spw->wxz", products, placing, precision=highest)
        targets = c_cols[own_row_cols]
        choose = (targets[:, :, None] == window[None, None, :]).astype(jnp.float32)
        chosen = jnp.einsum("qkw,wxz->qkxz", choose, spread, precision=highest)
        row_terms = jnp.einsum(
            "qyx,qkyz->qkxz", own_tiles.astype(jnp.float32), chosen, precision=highest
        )
        local_index = own_row_cols - base_coarse
        return (total.at[local_index].add(row_terms), None)

    initial = jnp.zeros((3 * coarse_rows, c_cols.shape[1], tile_size, tile_size), jnp.float32)
    total = lax.scan(fine_row, initial, (a_tiles[:, 0], local_cols, p_tiles, own_cols))[0]
    center = total[coarse_rows : 2 * coarse_rows]
    for offset, side_block in ((-1, total[:coarse_rows]), (1, total[2 * coarse_rows :])):
        center = center + passed_along(side_block, "row", offset)
    result = lax.psum_scatter(center, "grp", scatter_dimension=1, tiled=True)
    return result


def solution(mesh):
    return jax.shard_map(
        body,
        mesh=mesh,
        in_specs=(
            P("row", "grp", None, None, None),
            P("row", "grp", None),
            P("row", None, None, None),
            P(),
            P(),
        ),
        out_specs=P("row", "grp", None, None),
        check_vma=False,
    )
```

profile of v0, /device:TPU:10, one launch (start us, length us, event | category | flops | bytes accessed | tf_op | source)
XLA Modules:
  0.0 507.1 jit_solution(12076174178579070466)
XLA Ops:
  6.5 3.6 collective-permute-start
  12.1 3.6 collective-permute-start.2
  20.0 14.9 %collective-permute-done = bf16[8,4,128,128]{3,2,1,0:T(8,128)(2,1)} collective-permute-done((bf16[8,4,128,128]{3,2,1,0:T(8,128)(2,1)}, bf16[8,4,128,128]{3,2,1,0:T(8,128)(2,1)}, u32[]{:S(2)}, u32[]{:S(2)}) %collective-permute-start) | collective-permute-done | bytes 1048608 | tf_op jit(solution)/shard_map/ppermute | solution.py:15
  34.9 2.4 constant_dynamic-update-slice_fusion.4
  37.3 7.7 %collective-permute-done.1 = bf16[8,4,128,128]{3,2,1,0:T(8,128)(2,1)} collective-permute-done((bf16[8,4,128,128]{3,2,1,0:T(8,128)(2,1)}, bf16[8,4,128,128]{3,2,1,0:T(8,128)(2,1)}, u32[]{:S(2)}, u32[]{:S(2)}) %collective-permute-start.1) | collective-permute-done | bytes 1048608 | tf_op jit(solution)/shard_map/ppermute | solution.py:15
  45.0 2.3 constant_dynamic-update-slice_fusion.3
  48.4 2.3 constant_dynamic-update-slice_fusion.1
  50.7 2.0 collective-permute-done.3
  53.8 6.1 %broadcast_in_dim.2 = f32[12,16,128,128]{3,2,1,0:T(8,128)} broadcast(f32[]{:T(128)} %constant.10.clone.1), dimensions={} | broadcast | bytes 12582916 | tf_op jit(solution)/shard_map/broadcast_in_dim | solution.py:53
  59.9 273.8 %while.11 = (s32[]{:T(128)}, f32[12,16,128,128]{3,2,1,0:T(8,128)}, s32[8,4]{1,0:T(8,128)S(1)}, s32[]{:T(128)}, s32[32,16]{1,0:T(8,128)S(1)}, /*index=5*/s32[8,7]...) while((s32[]{:T(128)}, f32[12,16,128,128]{3,2,1,0:T(8,128)}, ...), condition=%wide.region_2.3_spmd.clone, body=%wide.region_0.2_spmd.clone.sunk | while | flops 2235568640 | bytes 51882804 | solution.py:54
  59.9 3.2 gather_fusion
  64.6 2.0 copy.34
  67.1 3.2 fusion.55
  72.7 7.1 %fusion.57 = f32[4,16,128,128]{2,3,1,0:T(8,128)} fusion(f32[4,16,128,128]{3,1,2,0:T(8,128)S(1)} %fusion.56, bf16[8,4,128,128]{3,2,1,0:T(8,128)(2,1)} %get-tuple-element.266, s32[]{:T(128)} %get-tuple-element.219), kind=kOutput, calls=%fused_computation.7.clone.1 | convolution fusion | flops 1610612736 | bytes 8520192 | tf_op jit(solution)/shard_map/while/body/eval_jaxpr/qyx,qkyz->qkxz/dot_general | solution.py:47
  79.8 5.3 %copy.35 = f32[4,16,128,128]{3,2,1,0:T(8,128)} copy(f32[4,16,128,128]{2,3,1,0:T(8,128)} %fusion.57) | data formatting | bytes 8388608 | tf_op jit(solution)/shard_map/while/body/eval_jaxpr/qyx,qkyz->qkxz/transpose | solution.py:47
  85.1 9.0 %scatter_fusion = f32[12,16,128,128]{3,2,1,0:T(8,128)} fusion(f32[12,16,128,128]{3,2,1,0:T(8,128)} %get-tuple-element.220, s32[4]{0:T(128)S(1)} %get-tuple-element.205, f32[4,16,128,128]{3,2,1,0:T(8,128)} %copy.35), kind=kCustom, calls=%fused_computation.3.clone.clone.1 | custom fusion | flops 1048576 | bytes 12582928 | tf_op jit(solution)/shard_map/while/body/eval_jaxpr/scatter-add | solution.py:51
  94.1 3.2 gather_fusion
  98.8 2.0 copy.34
  101.3 3.2 fusion.55
  107.0 7.1 %fusion.57 = f32[4,16,128,128]{2,3,1,0:T(8,128)} fusion(f32[4,16,128,128]{3,1,2,0:T(8,128)S(1)} %fusion.56, bf16[8,4,128,128]{3,2,1,0:T(8,128)(2,1)} %get-tuple-element.266, s32[]{:T(128)} %get-tuple-element.219), kind=kOutput, calls=%fused_computation.7.clone.1 | convolution fusion | flops 1610612736 | bytes 8520192 | tf_op jit(solution)/shard_map/while/body/eval_jaxpr/qyx,qkyz->qkxz/dot_general | solution.py:47
  114.0 5.3 %copy.35 = f32[4,16,128,128]{3,2,1,0:T(8,128)} copy(f32[4,16,128,128]{2,3,1,0:T(8,128)} %fusion.57) | data formatting | bytes 8388608 | tf_op jit(solution)/shard_map/while/body/eval_jaxpr/qyx,qkyz->qkxz/transpose | solution.py:47
  119.4 8.9 %scatter_fusion = f32[12,16,128,128]{3,2,1,0:T(8,128)} fusion(f32[12,16,128,128]{3,2,1,0:T(8,128)} %get-tuple-element.220, s32[4]{0:T(128)S(1)} %get-tuple-element.205, f32[4,16,128,128]{3,2,1,0:T(8,128)} %copy.35), kind=kCustom, calls=%fused_computation.3.clone.clone.1 | custom fusion | flops 1048576 | bytes 12582928 | tf_op jit(solution)/shard_map/while/body/eval_jaxpr/scatter-add | solution.py:51
  128.3 3.2 gather_fusion
  135.5 3.2 fusion.55
  141.1 7.1 %fusion.57 = f32[4,16,128,128]{2,3,1,0:T(8,128)} fusion(f32[4,16,128,128]{3,1,2,0:T(8,128)S(1)} %fusion.56, bf16[8,4,128,128]{3,2,1,0:T(8,128)(2,1)} %get-tuple-element.266, s32[]{:T(128)} %get-tuple-element.219), kind=kOutput, calls=%fused_computation.7.clone.1 | convolution fusion | flops 1610612736 | bytes 8520192 | tf_op jit(solution)/shard_map/while/body/eval_jaxpr/qyx,qkyz->qkxz/dot_general | solution.py:47
  148.2 5.3 %copy.35 = f32[4,16,128,128]{3,2,1,0:T(8,128)} copy(f32[4,16,128,128]{2,3,1,0:T(8,128)} %fusion.57) | data formatting | bytes 8388608 | tf_op jit(solution)/shard_map/while/body/eval_jaxpr/qyx,qkyz->qkxz/transpose | solution.py:47
  153.5 9.0 %scatter_fusion = f32[12,16,128,128]{3,2,1,0:T(8,128)} fusion(f32[12,16,128,128]{3,2,1,0:T(8,128)} %get-tuple-element.220, s32[4]{0:T(128)S(1)} %get-tuple-element.205, f32[4,16,128,128]{3,2,1,0:T(8,128)} %copy.35), kind=kCustom, calls=%fused_computation.3.clone.clone.1 | custom fusion | flops 1048576 | bytes 12582928 | tf_op jit(solution)/shard_map/while/body/eval_jaxpr/scatter-add | solution.py:51
  162.6 3.2 gather_fusion
  167.2 2.0 copy.34
  169.8 3.2 fusion.55
  175.4 7.1 %fusion.57 = f32[4,16,128,128]{2,3,1,0:T(8,128)} fusion(f32[4,16,128,128]{3,1,2,0:T(8,128)S(1)} %fusion.56, bf16[8,4,128,128]{3,2,1,0:T(8,128)(2,1)} %get-tuple-element.266, s32[]{:T(128)} %get-tuple-element.219), kind=kOutput, calls=%fused_computation.7.clone.1 | convolution fusion | flops 1610612736 | bytes 8520192 | tf_op jit(solution)/shard_map/while/body/eval_jaxpr/qyx,qkyz->qkxz/dot_general | solution.py:47
  182.4 5.3 %copy.35 = f32[4,16,128,128]{3,2,1,0:T(8,128)} copy(f32[4,16,128,128]{2,3,1,0:T(8,128)} %fusion.57) | data formatting | bytes 8388608 | tf_op jit(solution)/shard_map/while/body/eval_jaxpr/qyx,qkyz->qkxz/transpose | solution.py:47
  187.8 9.0 %scatter_fusion = f32[12,16,128,128]{3,2,1,0:T(8,128)} fusion(f32[12,16,128,128]{3,2,1,0:T(8,128)} %get-tuple-element.220, s32[4]{0:T(128)S(1)} %get-tuple-element.205, f32[4,16,128,128]{3,2,1,0:T(8,128)} %copy.35), kind=kCustom, calls=%fused_computation.3.clone.clone.1 | custom fusion | flops 1048576 | bytes 12582928 | tf_op jit(solution)/shard_map/while/body/eval_jaxpr/scatter-add | solution.py:51
  196.8 3.2 gather_fusion
  201.4 2.0 copy.34
  204.0 3.2 fusion.55
  209.6 7.1 %fusion.57 = f32[4,16,128,128]{2,3,1,0:T(8,128)} fusion(f32[4,16,128,128]{3,1,2,0:T(8,128)S(1)} %fusion.56, bf16[8,4,128,128]{3,2,1,0:T(8,128)(2,1)} %get-tuple-element.266, s32[]{:T(128)} %get-tuple-element.219), kind=kOutput, calls=%fused_computation.7.clone.1 | convolution fusion | flops 1610612736 | bytes 8520192 | tf_op jit(solution)/shard_map/while/body/eval_jaxpr/qyx,qkyz->qkxz/dot_general | solution.py:47
  216.7 5.3 %copy.35 = f32[4,16,128,128]{3,2,1,0:T(8,128)} copy(f32[4,16,128,128]{2,3,1,0:T(8,128)} %fusion.57) | data formatting | bytes 8388608 | tf_op jit(solution)/shard_map/while/body/eval_jaxpr/qyx,qkyz->qkxz/transpose | solution.py:47
  222.0 9.0 %scatter_fusion = f32[12,16,128,128]{3,2,1,0:T(8,128)} fusion(f32[12,16,128,128]{3,2,1,0:T(8,128)} %get-tuple-element.220, s32[4]{0:T(128)S(1)} %get-tuple-element.205, f32[4,16,128,128]{3,2,1,0:T(8,128)} %copy.35), kind=kCustom, calls=%fused_computation.3.clone.clone.1 | custom fusion | flops 1048576 | bytes 12582928 | tf_op jit(solution)/shard_map/while/body/eval_jaxpr/scatter-add | solution.py:51
  231.1 3.2 gather_fusion
  235.7 2.0 copy.34
  238.2 3.2 fusion.55
  243.9 7.1 %fusion.57 = f32[4,16,128,128]{2,3,1,0:T(8,128)} fusion(f32[4,16,128,128]{3,1,2,0:T(8,128)S(1)} %fusion.56, bf16[8,4,128,128]{3,2,1,0:T(8,128)(2,1)} %get-tuple-element.266, s32[]{:T(128)} %get-tuple-element.219), kind=kOutput, calls=%fused_computation.7.clone.1 | convolution fusion | flops 1610612736 | bytes 8520192 | tf_op jit(solution)/shard_map/while/body/eval_jaxpr/qyx,qkyz->qkxz/dot_general | solution.py:47
  250.9 5.3 %copy.35 = f32[4,16,128,128]{3,2,1,0:T(8,128)} copy(f32[4,16,128,128]{2,3,1,0:T(8,128)} %fusion.57) | data formatting | bytes 8388608 | tf_op jit(solution)/shard_map/while/body/eval_jaxpr/qyx,qkyz->qkxz/transpose | solution.py:47
  256.3 9.0 %scatter_fusion = f32[12,16,128,128]{3,2,1,0:T(8,128)} fusion(f32[12,16,128,128]{3,2,1,0:T(8,128)} %get-tuple-element.220, s32[4]{0:T(128)S(1)} %get-tuple-element.205, f32[4,16,128,128]{3,2,1,0:T(8,128)} %copy.35), kind=kCustom, calls=%fused_computation.3.clone.clone.1 | custom fusion | flops 1048576 | bytes 12582928 | tf_op jit(solution)/shard_map/while/body/eval_jaxpr/scatter-add | solution.py:51
  265.3 3.2 gather_fusion
  269.9 2.0 copy.34
  272.5 3.2 fusion.55
  278.1 7.1 %fusion.57 = f32[4,16,128,128]{2,3,1,0:T(8,128)} fusion(f32[4,16,128,128]{3,1,2,0:T(8,128)S(1)} %fusion.56, bf16[8,4,128,128]{3,2,1,0:T(8,128)(2,1)} %get-tuple-element.266, s32[]{:T(128)} %get-tuple-element.219), kind=kOutput, calls=%fused_computation.7.clone.1 | convolution fusion | flops 1610612736 | bytes 8520192 | tf_op jit(solution)/shard_map/while/body/eval_jaxpr/qyx,qkyz->qkxz/dot_general | solution.py:47
  285.2 5.3 %copy.35 = f32[4,16,128,128]{3,2,1,0:T(8,128)} copy(f32[4,16,128,128]{2,3,1,0:T(8,128)} %fusion.57) | data formatting | bytes 8388608 | tf_op jit(solution)/shard_map/while/body/eval_jaxpr/qyx,qkyz->qkxz/transpose | solution.py:47
  290.5 8.9 %scatter_fusion = f32[12,16,128,128]{3,2,1,0:T(8,128)} fusion(f32[12,16,128,128]{3,2,1,0:T(8,128)} %get-tuple-element.220, s32[4]{0:T(128)S(1)} %get-tuple-element.205, f32[4,16,128,128]{3,2,1,0:T(8,128)} %copy.35), kind=kCustom, calls=%fused_computation.3.clone.clone.1 | custom fusion | flops 1048576 | bytes 12582928 | tf_op jit(solution)/shard_map/while/body/eval_jaxpr/scatter-add | solution.py:51
  299.4 3.2 gather_fusion
  304.1 2.0 copy.34
  306.6 3.2 fusion.55
  312.3 7.1 %fusion.57 = f32[4,16,128,128]{2,3,1,0:T(8,128)} fusion(f32[4,16,128,128]{3,1,2,0:T(8,128)S(1)} %fusion.56, bf16[8,4,128,128]{3,2,1,0:T(8,128)(2,1)} %get-tuple-element.266, s32[]{:T(128)} %get-tuple-element.219), kind=kOutput, calls=%fused_computation.7.clone.1 | convolution fusion | flops 1610612736 | bytes 8520192 | tf_op jit(solution)/shard_map/while/body/eval_jaxpr/qyx,qkyz->qkxz/dot_general | solution.py:47
  319.3 5.3 %copy.35 = f32[4,16,128,128]{3,2,1,0:T(8,128)} copy(f32[4,16,128,128]{2,3,1,0:T(8,128)} %fusion.57) | data formatting | bytes 8388608 | tf_op jit(solution)/shard_map/while/body/eval_jaxpr/qyx,qkyz->qkxz/transpose | solution.py:47
  324.7 9.0 %scatter_fusion = f32[12,16,128,128]{3,2,1,0:T(8,128)} fusion(f32[12,16,128,128]{3,2,1,0:T(8,128)} %get-tuple-element.220, s32[4]{0:T(128)S(1)} %get-tuple-element.205, f32[4,16,128,128]{3,2,1,0:T(8,128)} %copy.35), kind=kCustom, calls=%fused_computation.3.clone.clone.1 | custom fusion | flops 1048576 | bytes 12582928 | tf_op jit(solution)/shard_map/while/body/eval_jaxpr/scatter-add | solution.py:51
  333.7 4.0 fusion.29
  339.7 2.4 collective-permute-start.5
  342.1 43.6 %collective-permute-done.4 = f32[4,16,128,128]{3,2,1,0:T(8,128)S(1)} collective-permute-done((f32[4,16,128,128]{3,2,1,0:T(8,128)S(1)}, f32[4,16,128,128]{3,2,1,0:T(8,128)S(1)}, u32[]{:S(2)}, u32[]{:S(2)}) %collective-permute-start.4) | collective-permute-done | bytes 4194336 | tf_op jit(solution)/shard_map/ppermute | solution.py:15
  385.7 3.8 collective-permute-done.5
  389.5 5.5 %add_add_fusion = f32[4,16,128,128]{3,2,1,0:T(8,128)} fusion(f32[4,16,128,128]{3,2,1,0:T(8,128)S(1)} %collective-permute-done.5, f32[4,16,128,128]{3,2,1,0:T(8,128)S(1)} %collective-permute-done.4, f32[12,16,128,128]{3,2,1,0:T(8,128)} %get-tuple-element.255), kind=kLoop, calls=%fused_computation.39 | loop fusion | flops 2097152 | bytes 16777216 | tf_op jit(solution)/shard_map/add | solution.py:57
  396.9 101.0 %all-reduce.4.cloned.1.call-done = f32[4,16,128,128]{3,2,1,0:T(8,128)} async-done(((f32[4,16,128,128]{3,2,1,0:T(8,128)}), f32[4,16,128,128]{3,2,1,0:T(8,128)}) %all-reduce.4.cloned.1.call-update) | async-done | bytes 4194320
  497.9 2.3 constant_dynamic-slice_fusion.2
  (108 shorter events, 48.9 us)
Async XLA Ops:
  6.5 40.8 %copy-start = (bf16[8,4,128,128]{3,2,1,0:T(8,128)(2,1)S(1)}, bf16[8,4,128,128]{3,2,1,0:T(8,128)(2,1)}, u32[]{:S(2)}) copy-start(bf16[8,4,128,128]{3,2,1,0:T(8,128)(2,1)} %param.9) | copy-start | bytes 3145732
  6.5 491.4 %all-reduce.4.cloned.1.call-start = ((), (), s32[]{:S(2)}) async-start(), calls=%async_computation | async-start | bytes 8388608
  6.5 28.4 %collective-permute-start = (bf16[8,4,128,128]{3,2,1,0:T(8,128)(2,1)}, bf16[8,4,128,128]{3,2,1,0:T(8,128)(2,1)}, u32[]{:S(2)}, u32[]{:S(2)}) collective-permute-start(bf16[8,4,128,128]{3,2,1,0:T(8,128)(2,1)} %param.9), channel_id=1, source_target_pairs={{0,2},{1,3},{2,4},{3,5},{4,6},{5,7},{8,10},{9,11},{10,12},{11,13},... | collective-permute-start | bytes 3145736 | tf_op jit(solution)/shard_map/ppermute | solution.py:15
  10.2 34.9 %collective-permute-start.1 = (bf16[8,4,128,128]{3,2,1,0:T(8,128)(2,1)}, bf16[8,4,128,128]{3,2,1,0:T(8,128)(2,1)}, u32[]{:S(2)}, u32[]{:S(2)}) collective-permute-start(bf16[8,4,128,128]{3,2,1,0:T(8,128)(2,1)} %param.9), channel_id=1, source_target_pairs={{0,1},{1,2},{2,3},{3,4},{4,5},{5,6},{6,7},{8,9},{9,10},{10,11},{11... | collective-permute-start | bytes 3145736 | tf_op jit(solution)/shard_map/ppermute | solution.py:15
  12.1 36.3 %collective-permute-start.2 = (bf16[8,4,128,128]{3,2,1,0:T(8,128)(2,1)}, bf16[8,4,128,128]{3,2,1,0:T(8,128)(2,1)}, u32[]{:S(2)}, u32[]{:S(2)}) collective-permute-start(bf16[8,4,128,128]{3,2,1,0:T(8,128)(2,1)} %param.9), channel_id=1, source_target_pairs={{1,0},{2,1},{3,2},{4,3},{5,4},{6,5},{7,6},{9,8},{10,9},{11,10},{12... | collective-permute-start | bytes 3145736 | tf_op jit(solution)/shard_map/ppermute | solution.py:15
  15.7 37.0 %collective-permute-start.3 = (bf16[8,4,128,128]{3,2,1,0:T(8,128)(2,1)}, bf16[8,4,128,128]{3,2,1,0:T(8,128)(2,1)S(1)}, u32[]{:S(2)}, u32[]{:S(2)}) collective-permute-start(bf16[8,4,128,128]{3,2,1,0:T(8,128)(2,1)} %param.9), channel_id=1, source_target_pairs={{2,0},{3,1},{4,2},{5,3},{6,4},{7,5},{10,8},{11,9},{12,10},{13,11},... | collective-permute-start | bytes 3145736 | tf_op jit(solution)/shard_map/ppermute | solution.py:15
  85.1 9.0 %copy-start.1 = (bf16[8,4,128,128]{3,2,1,0:T(8,128)(2,1)S(1)}, bf16[8,4,128,128]{3,2,1,0:T(8,128)(2,1)}, u32[]{:S(2)}) copy-start(bf16[8,4,128,128]{3,2,1,0:T(8,128)(2,1)} %get-tuple-element.266) | copy-start | bytes 3145732 | tf_op jit(solution)/shard_map/while
  119.4 8.9 %copy-start.1 = (bf16[8,4,128,128]{3,2,1,0:T(8,128)(2,1)S(1)}, bf16[8,4,128,128]{3,2,1,0:T(8,128)(2,1)}, u32[]{:S(2)}) copy-start(bf16[8,4,128,128]{3,2,1,0:T(8,128)(2,1)} %get-tuple-element.266) | copy-start | bytes 3145732 | tf_op jit(solution)/shard_map/while
  153.5 9.0 %copy-start.1 = (bf16[8,4,128,128]{3,2,1,0:T(8,128)(2,1)S(1)}, bf16[8,4,128,128]{3,2,1,0:T(8,128)(2,1)}, u32[]{:S(2)}) copy-start(bf16[8,4,128,128]{3,2,1,0:T(8,128)(2,1)} %get-tuple-element.266) | copy-start | bytes 3145732 | tf_op jit(solution)/shard_map/while
  187.8 9.0 %copy-start.1 = (bf16[8,4,128,128]{3,2,1,0:T(8,128)(2,1)S(1)}, bf16[8,4,128,128]{3,2,1,0:T(8,128)(2,1)}, u32[]{:S(2)}) copy-start(bf16[8,4,128,128]{3,2,1,0:T(8,128)(2,1)} %get-tuple-element.266) | copy-start | bytes 3145732 | tf_op jit(solution)/shard_map/while
  222.0 9.0 %copy-start.1 = (bf16[8,4,128,128]{3,2,1,0:T(8,128)(2,1)S(1)}, bf16[8,4,128,128]{3,2,1,0:T(8,128)(2,1)}, u32[]{:S(2)}) copy-start(bf16[8,4,128,128]{3,2,1,0:T(8,128)(2,1)} %get-tuple-element.266) | copy-start | bytes 3145732 | tf_op jit(solution)/shard_map/while
  256.3 9.0 %copy-start.1 = (bf16[8,4,128,128]{3,2,1,0:T(8,128)(2,1)S(1)}, bf16[8,4,128,128]{3,2,1,0:T(8,128)(2,1)}, u32[]{:S(2)}) copy-start(bf16[8,4,128,128]{3,2,1,0:T(8,128)(2,1)} %get-tuple-element.266) | copy-start | bytes 3145732 | tf_op jit(solution)/shard_map/while
  290.5 8.9 %copy-start.1 = (bf16[8,4,128,128]{3,2,1,0:T(8,128)(2,1)S(1)}, bf16[8,4,128,128]{3,2,1,0:T(8,128)(2,1)}, u32[]{:S(2)}) copy-start(bf16[8,4,128,128]{3,2,1,0:T(8,128)(2,1)} %get-tuple-element.266) | copy-start | bytes 3145732 | tf_op jit(solution)/shard_map/while
  324.6 9.0 %copy-start.1 = (bf16[8,4,128,128]{3,2,1,0:T(8,128)(2,1)S(1)}, bf16[8,4,128,128]{3,2,1,0:T(8,128)(2,1)}, u32[]{:S(2)}) copy-start(bf16[8,4,128,128]{3,2,1,0:T(8,128)(2,1)} %get-tuple-element.266) | copy-start | bytes 3145732 | tf_op jit(solution)/shard_map/while
  337.7 47.9 %collective-permute-start.4 = (f32[4,16,128,128]{3,2,1,0:T(8,128)S(1)}, f32[4,16,128,128]{3,2,1,0:T(8,128)S(1)}, u32[]{:S(2)}, u32[]{:S(2)}) collective-permute-start(f32[4,16,128,128]{3,2,1,0:T(8,128)S(1)} %get-tuple-element.134), channel_id=1, source_target_pairs={{1,0},{2,1},{3,2},{4,3},{5,4},{6,5},{7,6},{9,8},{10,9},{11,10},{12... | collective-permute-start | bytes 12582920 | tf_op jit(solution)/shard_map/ppermute | solution.py:15
  339.7 49.8 %collective-permute-start.5 = (f32[4,16,128,128]{3,2,1,0:T(8,128)S(1)}, f32[4,16,128,128]{3,2,1,0:T(8,128)S(1)}, u32[]{:S(2)}, u32[]{:S(2)}) collective-permute-start(f32[4,16,128,128]{3,2,1,0:T(8,128)S(1)} %get-tuple-element.135), channel_id=1, source_target_pairs={{0,1},{1,2},{2,3},{3,4},{4,5},{5,6},{6,7},{8,9},{9,10},{10,11},{11... | collective-permute-start | bytes 12582920 | tf_op jit(solution)/shard_map/ppermute | solution.py:15
  395.0 0.7 copy-start.2
Sparse Core Ops, SparseCore 0:
  395.2 102.7 all-reduce.3
where the time goes:
time: 511 us; the launch traced here: 507 us
  waiting for transfers between devices  173 us (34%)
  local copies, waits for them, and re-layouts  118 us (23%)
  matrix products  108 us (21%)
  other arithmetic  77.7 us (15%)
  starting transfers between devices  15.4 us (3%)
  between operations  14.1 us (3%)
    unnamed x2, waiting for transfers between devices  101 us
    ppermute x6, waiting for transfers between devices, passed_along(): return lax.ppermute(x, axis, pairs)  72.1 us
    scatter-add x8, other arithmetic, fine_row(): return (total.at[local_index].add(row_terms), None)  71.8 us
    dot_general x8, matrix products, fine_row(): jnp.einsum('qyx,qkyz->qkxz', own_tiles.astype(jnp.float32), chosen, preci...  56.5 us
    transpose x8, local copies, waits for them, and re-layouts, fine_row(): jnp.einsum('qyx,qkyz->qkxz', own_tiles.astype(jnp.float32), chosen, preci...  42.6 us
    gather x8, local copies, waits for them, and re-layouts, fine_row(): fetched = band_tiles[local_row]  25.7 us
    dot_general x8, matrix products, fine_row(): spread = jnp.einsum('spxz,spw->wxz', products, placing, precision=highest)  25.3 us
    transpose x8, local copies, waits for them, and re-layouts, fine_row(): jnp.einsum('sxy,spyz->spxz', a_row, fetched, preferred_element_type=jnp.f...  15.8 us
  transfers between devices with their start and end apart: 7, of which 6 were waited for; matrix products, arithmetic and copies ran while one was open for 2% of the time, Pallas kernels for 0%

commit v1 on v0

v1 whole, which is shorter than its diff:
```python
import functools

import jax
import jax.numpy as jnp
from jax import lax
from jax.experimental import pallas as pl
from jax.experimental.pallas import tpu as pltpu
from jax.sharding import PartitionSpec as P

RATIO = 2
REACH = 2


def passed_along(x, axis, by):
    size = lax.axis_size(axis)
    pairs = [(i, i + by) for i in range(size) if 0 <= i + by < size]
    return lax.ppermute(x, axis, pairs)


def product_kernel(
    sizes, where, a_cols, p_cols, c_cols, a_ref, band_ref, total_ref, spread, halves
):
    fine_rows, slots, kp, kc, tile = sizes
    coarse_rows = fine_rows // RATIO
    window = (2 * (REACH + 1) + 1) * coarse_rows
    position = where[0]
    first_row = position * fine_rows
    band_start = first_row - REACH * fine_rows
    window_start = (position - REACH - 1) * coarse_rows
    base_coarse = (position - 1) * coarse_rows
    total_ref[...] = jnp.zeros_like(total_ref)
    halves[window] = jnp.zeros((2 * tile, tile), jnp.bfloat16)
    group = min(4, kc)

    @pl.loop(0, fine_rows)
    def _(i):
        spread[...] = jnp.zeros_like(spread)
        for s in range(slots):
            j = a_cols[i * slots + s]
            local = (j - band_start) * kp
            right = jnp.concatenate([band_ref[local + p] for p in range(kp)], axis=1)
            prod = jnp.dot(a_ref[i * slots + s], right, preferred_element_type=jnp.float32)
            for p in range(kp):
                w = p_cols[j * kp + p] - window_start
                spread[w] = spread[w] + prod[:, p * tile : (p + 1) * tile]

        @pl.loop(0, window, unroll=4)
        def _(w):
            value = spread[w]
            high = value.astype(jnp.bfloat16)
            halves[w, :tile] = high
            halves[w, tile:] = (value - high.astype(jnp.float32)).astype(jnp.bfloat16)

        for q in range(kp):
            c = p_cols[(first_row + i) * kp + q]
            own = band_ref[(REACH * fine_rows + i) * kp + q].T
            left = jnp.concatenate([own, own], axis=1)
            out = (c - base_coarse) * kc
            for k in range(0, kc, group):
                parts = []
                for n in range(group):
                    w = c_cols[c * kc + k + n] - window_start
                    w = jnp.where((w < 0) | (w >= window), window, w)
                    parts.append(halves[w])
                prod = jnp.dot(
                    left, jnp.concatenate(parts, axis=1), preferred_element_type=jnp.float32
                )
                for n in range(group):
                    at = out + k + n
                    total_ref[at] = total_ref[at] + prod[:, n * tile : (n + 1) * tile]


def local_products(a_tiles, a_cols, band, p_cols, c_cols, position):
    fine_rows, _, slots, tile, _ = a_tiles.shape
    kp = band.shape[1]
    kc = c_cols.shape[1]
    coarse_rows = fine_rows // RATIO
    window = (2 * (REACH + 1) + 1) * coarse_rows
    smem = pl.BlockSpec(memory_space=pltpu.SMEM)
    vmem = pl.BlockSpec(memory_space=pltpu.VMEM)
    return pl.pallas_call(
        functools.partial(product_kernel, (fine_rows, slots, kp, kc, tile)),
        out_shape=jax.ShapeDtypeStruct((3 * coarse_rows * kc, tile, tile), jnp.float32),
        in_specs=[smem] * 4 + [vmem] * 2,
        out_specs=vmem,
        scratch_shapes=[
            pltpu.VMEM((window, tile, tile), jnp.float32),
            pltpu.VMEM((window + 1, 2 * tile, tile), jnp.bfloat16),
        ],
        compiler_params=pltpu.CompilerParams(vmem_limit_bytes=56 * 1024 * 1024),
    )(
        position.reshape(1),
        a_cols.reshape(-1),
        p_cols.reshape(-1),
        c_cols.reshape(-1),
        a_tiles.reshape(-1, tile, tile),
        band.reshape(-1, tile, tile),
    )


def body(a_tiles, a_cols, p_tiles, p_cols, c_cols):
    fine_rows = a_tiles.shape[0]
    coarse_rows = fine_rows // RATIO
    tile = a_tiles.shape[-1]
    kc = c_cols.shape[1]
    position = lax.axis_index("row")
    fetched = [passed_along(p_tiles, "row", offset) for offset in (2, 1, -1, -2)]
    band = jnp.concatenate([fetched[0], fetched[1], p_tiles, fetched[2], fetched[3]], axis=0)
    total = local_products(a_tiles, a_cols, band, p_cols, c_cols, position)
    total = total.reshape(3, coarse_rows, kc, tile, tile)
    center = total[1] + passed_along(total[0], "row", -1) + passed_along(total[2], "row", 1)
    return lax.psum_scatter(center, "grp", scatter_dimension=1, tiled=True)


def solution(mesh):
    return jax.shard_map(
        body,
        mesh=mesh,
        in_specs=(
            P("row", "grp", None, None, None),
            P("row", "grp", None),
            P("row", None, None, None),
            P(),
            P(),
        ),
        out_specs=P("row", "grp", None, None),
        check_vma=False,
    )
```

time: 511 us -> 255 us (0.50)
  matrix products: 108 us -> 0 us
  local copies, waits for them, and re-layouts: 118 us -> 23.6 us
  other arithmetic: 77.7 us -> 3.4 us
  Pallas kernels: 0 us -> 21.1 us
    dot_general x32 -> x0, matrix products: 108 us -> none  [the longest x8 56.5 us: fine_row(): jnp.einsum('qyx,qkyz->qkxz', own_tiles.astype(jnp.float32), chosen, preci...]
    scatter-add x8 -> x0, other arithmetic: 71.8 us -> none  [fine_row(): return (total.at[local_index].add(row_terms), None)]
    transpose x16 -> x0, local copies, waits for them, and re-layouts: 58.5 us -> none  [the longest x8 42.6 us: fine_row(): jnp.einsum('qyx,qkyz->qkxz', own_tiles.astype(jnp.float32), chosen, preci...]
    gather x24 -> x0, local copies, waits for them, and re-layouts: 34.6 us -> none  [the longest x8 25.7 us: fine_row(): fetched = band_tiles[local_row]]
    pallas_call x0 -> x1, Pallas kernels: none -> 21.1 us  [local_products(): pl.pallas_call(functools.partial(product_kernel, (fine_rows, slots, kp, k...]
    broadcast_in_dim x1 -> x0, local copies, waits for them, and re-layouts: 6.11 us -> none  [body(): jnp.zeros((3 * coarse_rows, c_cols.shape[1], tile_size, tile_size), jnp.f...]
    slice x1, local copies, waits for them, and re-layouts: 4.05 us -> 9.67 us  [body(): total[0]]
  transfers between devices with their start and end apart: 7 -> 7, of which waited for: 6 -> 6; matrix products, arithmetic and copies ran while one was open for 2% -> 4% of each run, Pallas kernels for 0% -> 0%
where the time goes in v1:
time: 255 us; the launch traced here: 253 us
  waiting for transfers between devices  176 us (69%)
  local copies, waits for them, and re-layouts  23.6 us (9%)
  Pallas kernels  21.1 us (8%)
  starting transfers between devices  15.3 us (6%)
  between operations  14.2 us (6%)
  other arithmetic  3.4 us (1%)
    unnamed x2, waiting for transfers between devices  102 us
    ppermute x6, waiting for transfers between devices, passed_along(): return lax.ppermute(x, axis, pairs)  74 us
    pallas_call x1, Pallas kernels, local_products(): pl.pallas_call(functools.partial(product_kernel, (fine_rows, slots, kp, k...  21.1 us
    ppermute x6, starting transfers between devices, passed_along(): return lax.ppermute(x, axis, pairs)  15.3 us
    unnamed x13, local copies, waits for them, and re-layouts  11.7 us
    slice x1, local copies, waits for them, and re-layouts, body(): total[0]  9.67 us
  transfers between devices with their start and end apart: 7, of which 6 were waited for; matrix products, arithmetic and copies ran while one was open for 4% of the time, Pallas kernels for 0%

profile of v1, /device:TPU:10, one launch (start us, length us, event | category | flops | bytes accessed | tf_op | source)
XLA Modules:
  0.0 253.2 jit_solution(11353950348054621297)
XLA Ops:
  6.5 0.0 all-reduce.3.cloned.1.call-start
  6.5 3.5 %collective-permute-start = (bf16[8,4,128,128]{3,2,1,0:T(8,128)(2,1)}, bf16[8,4,128,128]{3,2,1,0:T(8,128)(2,1)}, u32[]{:S(2)}, u32[]{:S(2)}) collective-permute-start(bf16[8,4,128,128]{3,2,1,0:T(8,128)(2,1)} %param.7), channel_id=1, source_target_pairs={{0,2},{1,3},{2,4},{3,5},{4,6},{5,7},{8,10},{9,11},{10,12},{11,13},... | collective-permute-start | bytes 3145736 | tf_op jit(solution)/shard_map/ppermute | solution.py:17
  10.0 1.9 collective-permute-start.1
  12.0 3.6 %collective-permute-start.2 = (bf16[8,4,128,128]{3,2,1,0:T(8,128)(2,1)}, bf16[8,4,128,128]{3,2,1,0:T(8,128)(2,1)S(1)}, u32[]{:S(2)}, u32[]{:S(2)}) collective-permute-start(bf16[8,4,128,128]{3,2,1,0:T(8,128)(2,1)} %param.7), channel_id=1, source_target_pairs={{1,0},{2,1},{3,2},{4,3},{5,4},{6,5},{7,6},{9,8},{10,9},{11,10},{12... | collective-permute-start | bytes 3145736 | tf_op jit(solution)/shard_map/ppermute | solution.py:17
  15.6 1.9 collective-permute-start.3
  17.5 0.8 copy.11
  18.3 0.7 reshape.27.p_cols
  19.0 0.8 copy.12
  19.8 0.7 reshape.28.c_cols
  20.4 0.8 copy.10
  21.2 0.7 reshape.26.a_cols
  21.9 12.9 %collective-permute-done = bf16[8,4,128,128]{3,2,1,0:T(8,128)(2,1)} collective-permute-done((bf16[8,4,128,128]{3,2,1,0:T(8,128)(2,1)}, bf16[8,4,128,128]{3,2,1,0:T(8,128)(2,1)}, u32[]{:S(2)}, u32[]{:S(2)}) %collective-permute-start) | collective-permute-done | bytes 1048608 | tf_op jit(solution)/shard_map/ppermute | solution.py:17
  34.8 1.3 constant_dynamic-update-slice_fusion.4
  36.1 8.8 %collective-permute-done.1 = bf16[8,4,128,128]{3,2,1,0:T(8,128)(2,1)} collective-permute-done((bf16[8,4,128,128]{3,2,1,0:T(8,128)(2,1)}, bf16[8,4,128,128]{3,2,1,0:T(8,128)(2,1)}, u32[]{:S(2)}, u32[]{:S(2)}) %collective-permute-start.1) | collective-permute-done | bytes 1048608 | tf_op jit(solution)/shard_map/ppermute | solution.py:17
  44.9 1.4 constant_dynamic-update-slice_fusion.3
  46.3 1.4 constant_dynamic-update-slice_fusion.2
  47.7 0.0 collective-permute-done.2
  47.7 0.2 constant_dynamic-update-slice_fusion.1
  47.9 4.7 %collective-permute-done.3 = bf16[8,4,128,128]{3,2,1,0:T(8,128)(2,1)S(1)} collective-permute-done((bf16[8,4,128,128]{3,2,1,0:T(8,128)(2,1)}, bf16[8,4,128,128]{3,2,1,0:T(8,128)(2,1)S(1)}, u32[]{:S(2)}, u32[]{:S(2)}) %collective-permute-start.3) | collective-permute-done | bytes 1048608 | tf_op jit(solution)/shard_map/ppermute | solution.py:17
  52.6 0.2 constant_dynamic-update-slice_fusion
  52.8 0.0 copy-start
  52.8 2.2 copy-done
  55.0 21.1 %shard_map.55 = f32[192,128,128]{2,1,0:T(8,128)} custom-call(s32[1]{0:T(128)} %bitcast.6.where, s32[56]{0:T(128)} %reshape.26.a_cols, s32[256]{0:T(256)} %reshape.27.p_cols, s32[512]{0:T(512)} %reshape.28.c_cols, bf16[56,128,128]{2,1,0:T(8,128)(2,1)} %bitcast.19, bf16[160,128,128]{2,1,0:T(8,128)(2,1)} %bitcast.16), custom_call_target="tpu_custom_call" | custom-call | tf_op jit(solution)/shard_map/pallas_call | solution.py:81
  76.1 9.7 %fusion = (f32[64,128,128]{2,1,0:T(8,128)}, f32[64,128,128]{2,1,0:T(8,128)}, f32[64,128,128]{2,1,0:T(8,128)S(1)}) fusion(f32[192,128,128]{2,1,0:T(8,128)} %shard_map.55), kind=kLoop, calls=%fused_computation.7 | loop fusion | bytes 25165824 | tf_op jit(solution)/shard_map/slice | solution.py:111
  85.8 1.9 collective-permute-start.4
  87.7 2.4 collective-permute-start.5
  90.1 43.9 %collective-permute-done.4 = f32[4,16,128,128]{3,2,1,0:T(8,128)S(1)} collective-permute-done((f32[4,16,128,128]{3,2,1,0:T(8,128)}, f32[4,16,128,128]{3,2,1,0:T(8,128)S(1)}, u32[]{:S(2)}, u32[]{:S(2)}) %collective-permute-start.4) | collective-permute-done | bytes 4194336 | tf_op jit(solution)/shard_map/ppermute | solution.py:17
  134.0 3.7 %collective-permute-done.5 = f32[4,16,128,128]{3,2,1,0:T(8,128)S(1)} collective-permute-done((f32[4,16,128,128]{3,2,1,0:T(8,128)}, f32[4,16,128,128]{3,2,1,0:T(8,128)S(1)}, u32[]{:S(2)}, u32[]{:S(2)}) %collective-permute-start.5) | collective-permute-done | bytes 4194336 | tf_op jit(solution)/shard_map/ppermute | solution.py:17
  137.7 0.0 copy-start.1
  137.7 3.4 %add_add_fusion = f32[4,16,128,128]{3,2,1,0:T(8,128)} fusion(f32[4,16,128,128]{3,2,1,0:T(8,128)S(1)} %collective-permute-done.5, f32[4,16,128,128]{3,2,1,0:T(8,128)S(1)} %bitcast.15, f32[4,16,128,128]{3,2,1,0:T(8,128)S(1)} %collective-permute-done.4), kind=kLoop, calls=%fused_computation | loop fusion | flops 2097152 | bytes 16777216 | tf_op jit(solution)/shard_map/add | solution.py:111
  141.1 0.0 all-reduce.3.cloned.1.call-update
  141.2 0.0 copy-done.1
  141.2 0.6 dynamic-slice
  142.4 101.6 %all-reduce.3.cloned.1.call-done = f32[4,16,128,128]{3,2,1,0:T(8,128)} async-done(((f32[4,16,128,128]{3,2,1,0:T(8,128)}), f32[4,16,128,128]{3,2,1,0:T(8,128)}) %all-reduce.3.cloned.1.call-update) | async-done | bytes 4194320
  244.0 2.3 constant_dynamic-slice_fusion
Async XLA Ops:
  6.5 237.5 %all-reduce.3.cloned.1.call-start = ((), (), s32[]{:S(2)}) async-start(), calls=%async_computation | async-start | bytes 8388608
  6.5 28.2 %collective-permute-start = (bf16[8,4,128,128]{3,2,1,0:T(8,128)(2,1)}, bf16[8,4,128,128]{3,2,1,0:T(8,128)(2,1)}, u32[]{:S(2)}, u32[]{:S(2)}) collective-permute-start(bf16[8,4,128,128]{3,2,1,0:T(8,128)(2,1)} %param.7), channel_id=1, source_target_pairs={{0,2},{1,3},{2,4},{3,5},{4,6},{5,7},{8,10},{9,11},{10,12},{11,13},... | collective-permute-start | bytes 3145736 | tf_op jit(solution)/shard_map/ppermute | solution.py:17
  10.0 34.9 %collective-permute-start.1 = (bf16[8,4,128,128]{3,2,1,0:T(8,128)(2,1)}, bf16[8,4,128,128]{3,2,1,0:T(8,128)(2,1)}, u32[]{:S(2)}, u32[]{:S(2)}) collective-permute-start(bf16[8,4,128,128]{3,2,1,0:T(8,128)(2,1)} %param.7), channel_id=1, source_target_pairs={{0,1},{1,2},{2,3},{3,4},{4,5},{5,6},{6,7},{8,9},{9,10},{10,11},{11... | collective-permute-start | bytes 3145736 | tf_op jit(solution)/shard_map/ppermute | solution.py:17
  12.0 35.7 %collective-permute-start.2 = (bf16[8,4,128,128]{3,2,1,0:T(8,128)(2,1)}, bf16[8,4,128,128]{3,2,1,0:T(8,128)(2,1)S(1)}, u32[]{:S(2)}, u32[]{:S(2)}) collective-permute-start(bf16[8,4,128,128]{3,2,1,0:T(8,128)(2,1)} %param.7), channel_id=1, source_target_pairs={{1,0},{2,1},{3,2},{4,3},{5,4},{6,5},{7,6},{9,8},{10,9},{11,10},{12... | collective-permute-start | bytes 3145736 | tf_op jit(solution)/shard_map/ppermute | solution.py:17
  15.6 37.0 %collective-permute-start.3 = (bf16[8,4,128,128]{3,2,1,0:T(8,128)(2,1)}, bf16[8,4,128,128]{3,2,1,0:T(8,128)(2,1)S(1)}, u32[]{:S(2)}, u32[]{:S(2)}) collective-permute-start(bf16[8,4,128,128]{3,2,1,0:T(8,128)(2,1)} %param.7), channel_id=1, source_target_pairs={{2,0},{3,1},{4,2},{5,3},{6,4},{7,5},{10,8},{11,9},{12,10},{13,11},... | collective-permute-start | bytes 3145736 | tf_op jit(solution)/shard_map/ppermute | solution.py:17
  52.8 2.3 copy-start
  85.8 48.2 %collective-permute-start.4 = (f32[4,16,128,128]{3,2,1,0:T(8,128)}, f32[4,16,128,128]{3,2,1,0:T(8,128)S(1)}, u32[]{:S(2)}, u32[]{:S(2)}) collective-permute-start(f32[4,16,128,128]{3,2,1,0:T(8,128)} %bitcast.18), channel_id=1, source_target_pairs={{1,0},{2,1},{3,2},{4,3},{5,4},{6,5},{7,6},{9,8},{10,9},{11,10},{12... | collective-permute-start | bytes 12582920 | tf_op jit(solution)/shard_map/ppermute | solution.py:17
  87.7 50.0 %collective-permute-start.5 = (f32[4,16,128,128]{3,2,1,0:T(8,128)}, f32[4,16,128,128]{3,2,1,0:T(8,128)S(1)}, u32[]{:S(2)}, u32[]{:S(2)}) collective-permute-start(f32[4,16,128,128]{3,2,1,0:T(8,128)} %bitcast.17), channel_id=1, source_target_pairs={{0,1},{1,2},{2,3},{3,4},{4,5},{5,6},{6,7},{8,9},{9,10},{10,11},{11... | collective-permute-start | bytes 12582920 | tf_op jit(solution)/shard_map/ppermute | solution.py:17
  137.7 3.4 %copy-start.1 = (u32[32]{0:T(128)S(1)}, u32[32]{0:T(128)}, u32[]{:S(2)}) copy-start(u32[32]{0:T(128)} %constant.8) | copy-start | bytes 388
Sparse Core Ops, SparseCore 0:
  141.3 102.7 all-reduce.2

commit v2 on v1

--- a/solution.py
+++ b/solution.py
@@ -17,10 +17,35 @@
     return lax.ppermute(x, axis, pairs)
 
 
+LEVELS = 32767.0
+
+
+def encoded(value):
+    most = jnp.maximum(jnp.max(jnp.abs(value), axis=0, keepdims=True), 2e-34)
+    code = jnp.round(value * (LEVELS / most)).astype(jnp.int32).astype(jnp.int16)
+    return code, most * (1.0 / LEVELS)
+
+
+def decoded(code, scale):
+    return code.astype(jnp.int32).astype(jnp.float32) * scale
+
+
 def product_kernel(
-    sizes, where, a_cols, p_cols, c_cols, a_ref, band_ref, total_ref, spread, halves
+    sizes,
+    where,
+    a_cols,
+    p_cols,
+    c_cols,
+    a_ref,
+    band_ref,
+    center_ref,
+    codes_ref,
+    scales_ref,
+    total_ref,
+    spread,
+    halves,
 ):
-    fine_rows, slots, kp, kc, tile = sizes
+    fine_rows, slots, kp, kc, tile, chunks = sizes
     coarse_rows = fine_rows // RATIO
     window = (2 * (REACH + 1) + 1) * coarse_rows
     position = where[0]
@@ -69,21 +94,42 @@
                     at = out + k + n
                     total_ref[at] = total_ref[at] + prod[:, n * tile : (n + 1) * tile]
 
-
-def local_products(a_tiles, a_cols, band, p_cols, c_cols, position):
+    share = kc // chunks
+    for chunk in range(chunks):
+
+        @pl.loop(0, coarse_rows)
+        def _(c):
+            for n in range(share):
+                e = c * share + n
+                k = chunk * share + n
+                center_ref[chunk, e] = total_ref[(coarse_rows + c) * kc + k]
+                for side in range(2):
+                    value = total_ref[(2 * side * coarse_rows + c) * kc + k]
+                    code, scale = encoded(value)
+                    codes_ref[side, chunk, e] = code
+                    scales_ref[side, chunk, pl.ds(e, 1)] = scale
+
+
+def local_products(a_tiles, a_cols, band, p_cols, c_cols, position, chunks):
     fine_rows, _, slots, tile, _ = a_tiles.shape
     kp = band.shape[1]
     kc = c_cols.shape[1]
     coarse_rows = fine_rows // RATIO
     window = (2 * (REACH + 1) + 1) * coarse_rows
+    members = coarse_rows * kc // chunks
     smem = pl.BlockSpec(memory_space=pltpu.SMEM)
     vmem = pl.BlockSpec(memory_space=pltpu.VMEM)
     return pl.pallas_call(
-        functools.partial(product_kernel, (fine_rows, slots, kp, kc, tile)),
-        out_shape=jax.ShapeDtypeStruct((3 * coarse_rows * kc, tile, tile), jnp.float32),
+        functools.partial(product_kernel, (fine_rows, slots, kp, kc, tile, chunks)),
+        out_shape=[
+            jax.ShapeDtypeStruct((chunks, members, tile, tile), jnp.float32),
+            jax.ShapeDtypeStruct((2, chunks, members, tile, tile), jnp.int16),
+            jax.ShapeDtypeStruct((2, chunks, members, tile), jnp.float32),
+        ],
         in_specs=[smem] * 4 + [vmem] * 2,
-        out_specs=vmem,
+        out_specs=[vmem] * 3,
         scratch_shapes=[
+            pltpu.VMEM((3 * coarse_rows * kc, tile, tile), jnp.float32),
             pltpu.VMEM((window, tile, tile), jnp.float32),
             pltpu.VMEM((window + 1, 2 * tile, tile), jnp.bfloat16),
         ],
@@ -98,18 +144,207 @@
     )
 
 
+def exchange_kernel(
+    rows,
+    chunks,
+    center,
+    codes,
+    scales,
+    out,
+    side_codes,
+    side_scales,
+    sent_codes,
+    sent_scales,
+    peer_codes,
+    peer_scales,
+    side_sems,
+    side_scale_sems,
+    peer_sems,
+    peer_scale_sems,
+):
+    r = lax.axis_index("row")
+    g = lax.axis_index("grp")
+    members = out.shape[0]
+    barrier = pltpu.get_barrier_semaphore()
+    mesh_type = pl.DeviceIdType.MESH
+
+    def signal(where):
+        pl.semaphore_signal(barrier, inc=1, device_id=where, device_id_type=mesh_type)
+
+    for t in range(chunks - 1):
+        signal({"grp": lax.rem(g + 1 + t, chunks)})
+
+    @pl.when(r > 0)
+    def _():
+        signal({"row": r - 1})
+
+    @pl.when(r < rows - 1)
+    def _():
+        signal({"row": r + 1})
+
+    inside = (r > 0) & (r < rows - 1)
+
+    @pl.when(inside)
+    def _():
+        pl.semaphore_wait(barrier, chunks + 1)
+
+    @pl.when(jnp.logical_not(inside))
+    def _():
+        pl.semaphore_wait(barrier, chunks)
+
+    sends = ((r > 0, r - 1), (r < rows - 1, r + 1))
+    comes = (r < rows - 1, r > 0)
+
+    def scale_copy(side):
+        return pltpu.make_async_remote_copy(
+            src_ref=scales.at[side],
+            dst_ref=side_scales.at[side],
+            send_sem=side_scale_sems.at[0, side],
+            recv_sem=side_scale_sems.at[1, side],
+            device_id={"row": sends[side][1]},
+            device_id_type=mesh_type,
+        )
+
+    def side_copy(side, t):
+        return pltpu.make_async_remote_copy(
+            src_ref=codes.at[side, lax.rem(g + 1 + t, chunks)],
+            dst_ref=side_codes.at[side, t],
+            send_sem=side_sems.at[0, side, t],
+            recv_sem=side_sems.at[1, side, t],
+            device_id={"row": sends[side][1]},
+            device_id_type=mesh_type,
+        )
+
+    def peer_copy(t):
+        return pltpu.make_async_remote_copy(
+            src_ref=sent_codes.at[t],
+            dst_ref=peer_codes.at[t],
+            send_sem=peer_sems.at[0, t],
+            recv_sem=peer_sems.at[1, t],
+            device_id={"grp": lax.rem(g + 1 + t, chunks)},
+            device_id_type=mesh_type,
+        )
+
+    def peer_scale_copy(t):
+        return pltpu.make_async_remote_copy(
+            src_ref=sent_scales.at[t],
+            dst_ref=peer_scales.at[t],
+            send_sem=peer_scale_sems.at[0, t],
+            recv_sem=peer_scale_sems.at[1, t],
+            device_id={"grp": lax.rem(g + 1 + t, chunks)},
+            device_id_type=mesh_type,
+        )
+
+    for side in range(2):
+
+        @pl.when(sends[side][0])
+        def _():
+            scale_copy(side).start()
+            for t in range(chunks):
+                side_copy(side, t).start()
+
+        @pl.when(jnp.logical_not(comes[side]))
+        def _():
+            side_scales[side] = jnp.zeros_like(side_scales[side])
+
+            @pl.loop(0, chunks)
+            def _(t):
+                @pl.loop(0, members)
+                def _(e):
+                    side_codes[side, t, e] = jnp.zeros(side_codes.shape[3:], jnp.int16)
+
+    for side in range(2):
+
+        @pl.when(comes[side])
+        def _():
+            scale_copy(side).wait_recv()
+
+    for t in range(chunks):
+        d = lax.rem(g + 1 + t, chunks)
+        for side in range(2):
+
+            @pl.when(comes[side])
+            def _():
+                side_copy(side, t).wait_recv()
+
+        @pl.loop(0, members)
+        def _(e):
+            value = center[d, e]
+            for side in range(2):
+                value += decoded(side_codes[side, t, e], side_scales[side, d, pl.ds(e, 1)])
+            if t < chunks - 1:
+                code, scale = encoded(value)
+                sent_codes[t, e] = code
+                sent_scales[t, pl.ds(e, 1)] = scale
+            else:
+                out[e] = value
+
+        if t < chunks - 1:
+            peer_scale_copy(t).start()
+            peer_copy(t).start()
+
+    for t in range(chunks - 1):
+        peer_scale_copy(t).wait_recv()
+        peer_copy(t).wait_recv()
+
+        @pl.loop(0, members)
+        def _(e):
+            out[e] = out[e] + decoded(peer_codes[t, e], peer_scales[t, pl.ds(e, 1)])
+
+    for t in range(chunks - 1):
+        peer_scale_copy(t).wait_send()
+        peer_copy(t).wait_send()
+    for side in range(2):
+
+        @pl.when(sends[side][0])
+        def _():
+            scale_copy(side).wait_send()
+            for t in range(chunks):
+                side_copy(side, t).wait_send()
+
+
+def exchange(center, codes, scales, rows):
+    chunks, members, tile, _ = center.shape
+    vmem = pl.BlockSpec(memory_space=pltpu.VMEM)
+    anywhere = pl.BlockSpec(memory_space=pl.ANY)
+    dma = pltpu.SemaphoreType.DMA
+    return pl.pallas_call(
+        functools.partial(exchange_kernel, rows, chunks),
+        out_shape=jax.ShapeDtypeStruct((members, tile, tile), jnp.float32),
+        in_specs=[vmem, anywhere, vmem],
+        out_specs=vmem,
+        scratch_shapes=[
+            pltpu.VMEM((2, chunks, members, tile, tile), jnp.int16),
+            pltpu.VMEM((2, chunks, members, tile), jnp.float32),
+            pltpu.VMEM((chunks - 1, members, tile, tile), jnp.int16),
+            pltpu.VMEM((chunks - 1, members, tile), jnp.float32),
+            pltpu.VMEM((chunks - 1, members, tile, tile), jnp.int16),
+            pltpu.VMEM((chunks - 1, members, tile), jnp.float32),
+            dma((2, 2, chunks)),
+            dma((2, 2)),
+            dma((2, chunks - 1)),
+            dma((2, chunks - 1)),
+        ],
+        compiler_params=pltpu.CompilerParams(
+            collective_id=0, has_side_effects=True, vmem_limit_bytes=40 * 1024 * 1024
+        ),
+    )(center, codes, scales)
+
+
 def body(a_tiles, a_cols, p_tiles, p_cols, c_cols):
     fine_rows = a_tiles.shape[0]
     coarse_rows = fine_rows // RATIO
     tile = a_tiles.shape[-1]
     kc = c_cols.shape[1]
+    chunks = lax.axis_size("grp")
     position = lax.axis_index("row")
     fetched = [passed_along(p_tiles, "row", offset) for offset in (2, 1, -1, -2)]
     band = jnp.concatenate([fetched[0], fetched[1], p_tiles, fetched[2], fetched[3]], axis=0)
-    total = local_products(a_tiles, a_cols, band, p_cols, c_cols, position)
-    total = total.reshape(3, coarse_rows, kc, tile, tile)
-    center = total[1] + passed_along(total[0], "row", -1) + passed_along(total[2], "row", 1)
-    return lax.psum_scatter(center, "grp", scatter_dimension=1, tiled=True)
+    center, codes, scales = local_products(
+        a_tiles, a_cols, band, p_cols, c_cols, position, chunks
+    )
+    out = exchange(center, codes, scales, lax.axis_size("row"))
+    return out.reshape(coarse_rows, kc // chunks, tile, tile)
 
 
 def solution(mesh):

time: 255 us -> 117 us (0.46)
  waiting for transfers between devices: 176 us -> 26.5 us
  Pallas kernels: 21.1 us -> 61.6 us
  between operations: 14.2 us -> 0.11 us
  local copies, waits for them, and re-layouts: 23.6 us -> 17.2 us
  starting transfers between devices: 15.3 us -> 11 us
  other arithmetic: 3.4 us -> 0 us
    unnamed x2 -> x0, waiting for transfers between devices: 102 us -> none
    ppermute x6 -> x4, waiting for transfers between devices: 74 us -> 26.5 us  [passed_along(): return lax.ppermute(x, axis, pairs)]
    pallas_call x0 -> x1, Pallas kernels: none -> 40.1 us  [exchange(): pl.pallas_call(functools.partial(exchange_kernel, rows, chunks), out_shap...]
    slice x1 -> x0, local copies, waits for them, and re-layouts: 9.67 us -> none  [body(): total[0]]
    ppermute x6 -> x4, starting transfers between devices: 15.3 us -> 11 us  [passed_along(): return lax.ppermute(x, axis, pairs)]
    add x1 -> x0, other arithmetic: 3.4 us -> none  [body(): total[1] + passed_along(total[0], 'row', -1)]
    unnamed x13 -> x16, local copies, waits for them, and re-layouts: 11.7 us -> 15.1 us
  transfers between devices with their start and end apart: 7 -> 4, of which waited for: 6 -> 3; matrix products, arithmetic and copies ran while one was open for 4% -> 7% of each run, Pallas kernels for 0% -> 0%
where the time goes in v2:
time: 117 us; the launch traced here: 116 us
  Pallas kernels  61.6 us (53%)
  waiting for transfers between devices  26.5 us (23%)
  local copies, waits for them, and re-layouts  17.2 us (15%)
  starting transfers between devices  11 us (9%)
    pallas_call x1, Pallas kernels, exchange(): pl.pallas_call(functools.partial(exchange_kernel, rows, chunks), out_shap...  40.1 us
    ppermute x4, waiting for transfers between devices, passed_along(): return lax.ppermute(x, axis, pairs)  26.5 us
    pallas_call x1, Pallas kernels, local_products(): pl.pallas_call(functools.partial(product_kernel, (fine_rows, slots, kp, k...  21.6 us
    unnamed x16, local copies, waits for them, and re-layouts  15.1 us
    ppermute x4, starting transfers between devices, passed_along(): return lax.ppermute(x, axis, pairs)  11 us
  transfers between devices with their start and end apart: 4, of which 3 were waited for; matrix products, arithmetic and copies ran while one was open for 7% of the time, Pallas kernels for 0%

profile of v2, /device:TPU:10, one launch (start us, length us, event | category | flops | bytes accessed | tf_op | source)
XLA Modules:
  0.0 116.4 jit_solution(8466653013365494134)
XLA Ops:
  0.0 3.5 %collective-permute-start = (bf16[8,4,128,128]{3,2,1,0:T(8,128)(2,1)}, bf16[8,4,128,128]{3,2,1,0:T(8,128)(2,1)}, u32[]{:S(2)}, u32[]{:S(2)}) collective-permute-start(bf16[8,4,128,128]{3,2,1,0:T(8,128)(2,1)} %param.7), channel_id=1, source_target_pairs={{0,2},{1,3},{2,4},{3,5},{4,6},{5,7},{8,10},{9,11},{10,12},{11,13},... | collective-permute-start | bytes 3145736 | tf_op jit(solution)/shard_map/ppermute | solution.py:17
  3.5 1.9 %collective-permute-start.1 = (bf16[8,4,128,128]{3,2,1,0:T(8,128)(2,1)}, bf16[8,4,128,128]{3,2,1,0:T(8,128)(2,1)}, u32[]{:S(2)}, u32[]{:S(2)}) collective-permute-start(bf16[8,4,128,128]{3,2,1,0:T(8,128)(2,1)} %param.7), channel_id=1, source_target_pairs={{0,1},{1,2},{2,3},{3,4},{4,5},{5,6},{6,7},{8,9},{9,10},{10,11},{11... | collective-permute-start | bytes 3145736 | tf_op jit(solution)/shard_map/ppermute | solution.py:17
  5.4 3.6 %collective-permute-start.2 = (bf16[8,4,128,128]{3,2,1,0:T(8,128)(2,1)}, bf16[8,4,128,128]{3,2,1,0:T(8,128)(2,1)S(1)}, u32[]{:S(2)}, u32[]{:S(2)}) collective-permute-start(bf16[8,4,128,128]{3,2,1,0:T(8,128)(2,1)} %param.7), channel_id=1, source_target_pairs={{1,0},{2,1},{3,2},{4,3},{5,4},{6,5},{7,6},{9,8},{10,9},{11,10},{12... | collective-permute-start | bytes 3145736 | tf_op jit(solution)/shard_map/ppermute | solution.py:17
  9.1 1.9 %collective-permute-start.3 = (bf16[8,4,128,128]{3,2,1,0:T(8,128)(2,1)}, bf16[8,4,128,128]{3,2,1,0:T(8,128)(2,1)S(1)}, u32[]{:S(2)}, u32[]{:S(2)}) collective-permute-start(bf16[8,4,128,128]{3,2,1,0:T(8,128)(2,1)} %param.7), channel_id=1, source_target_pairs={{2,0},{3,1},{4,2},{5,3},{6,4},{7,5},{10,8},{11,9},{12,10},{13,11},... | collective-permute-start | bytes 3145736 | tf_op jit(solution)/shard_map/ppermute | solution.py:17
  11.0 0.8 copy.7
  11.8 0.6 reshape.22.a_cols
  12.4 0.8 copy.9
  13.1 0.6 reshape.24.c_cols
  13.8 0.8 copy.8
  14.5 0.7 reshape.23.p_cols
  15.2 13.0 %collective-permute-done = bf16[8,4,128,128]{3,2,1,0:T(8,128)(2,1)} collective-permute-done((bf16[8,4,128,128]{3,2,1,0:T(8,128)(2,1)}, bf16[8,4,128,128]{3,2,1,0:T(8,128)(2,1)}, u32[]{:S(2)}, u32[]{:S(2)}) %collective-permute-start) | collective-permute-done | bytes 1048608 | tf_op jit(solution)/shard_map/ppermute | solution.py:17
  28.2 1.3 %constant_dynamic-update-slice_fusion.4 = bf16[40,4,128,128]{3,2,1,0:T(8,128)(2,1)S(1)} fusion(bf16[8,4,128,128]{3,2,1,0:T(8,128)(2,1)} %collective-permute-done), kind=kLoop, calls=%fused_computation.4 | loop fusion | bytes 2097152
  29.6 8.8 %collective-permute-done.1 = bf16[8,4,128,128]{3,2,1,0:T(8,128)(2,1)} collective-permute-done((bf16[8,4,128,128]{3,2,1,0:T(8,128)(2,1)}, bf16[8,4,128,128]{3,2,1,0:T(8,128)(2,1)}, u32[]{:S(2)}, u32[]{:S(2)}) %collective-permute-start.1) | collective-permute-done | bytes 1048608 | tf_op jit(solution)/shard_map/ppermute | solution.py:17
  38.3 1.4 %constant_dynamic-update-slice_fusion.3 = bf16[40,4,128,128]{3,2,1,0:T(8,128)(2,1)S(1)} fusion(bf16[40,4,128,128]{3,2,1,0:T(8,128)(2,1)S(1)} %constant_dynamic-update-slice_fusion.4, bf16[8,4,128,128]{3,2,1,0:T(8,128)(2,1)} %collective-permute-done.1), kind=kLoop, calls=%fused_computation.3 | loop fusion | bytes 2097152
  39.7 1.4 %constant_dynamic-update-slice_fusion.2 = bf16[40,4,128,128]{3,2,1,0:T(8,128)(2,1)S(1)} fusion(bf16[40,4,128,128]{3,2,1,0:T(8,128)(2,1)S(1)} %constant_dynamic-update-slice_fusion.3, bf16[8,4,128,128]{3,2,1,0:T(8,128)(2,1)} %param.7), kind=kLoop, calls=%fused_computation.2 | loop fusion | bytes 2097152
  41.2 0.0 collective-permute-done.2
  41.2 0.2 constant_dynamic-update-slice_fusion.1
  41.4 4.7 %collective-permute-done.3 = bf16[8,4,128,128]{3,2,1,0:T(8,128)(2,1)S(1)} collective-permute-done((bf16[8,4,128,128]{3,2,1,0:T(8,128)(2,1)}, bf16[8,4,128,128]{3,2,1,0:T(8,128)(2,1)S(1)}, u32[]{:S(2)}, u32[]{:S(2)}) %collective-permute-start.3) | collective-permute-done | bytes 1048608 | tf_op jit(solution)/shard_map/ppermute | solution.py:17
  46.1 0.2 constant_dynamic-update-slice_fusion
  46.3 0.0 copy-start.3
  46.3 2.3 %copy-done.3 = bf16[40,4,128,128]{3,2,1,0:T(8,128)(2,1)} copy-done((bf16[40,4,128,128]{3,2,1,0:T(8,128)(2,1)}, bf16[40,4,128,128]{3,2,1,0:T(8,128)(2,1)S(1)}, u32[]{:S(2)}) %copy-start.3) | copy-done | bytes 5242904
  48.6 21.6 %shard_map.55 = (f32[4,16,128,128]{3,2,1,0:T(8,128)}, s16[2,4,16,128,128]{4,3,2,1,0:T(8,128)(2,1)}, f32[2,4,16,128]{3,2,1,0:T(8,128)}) custom-call(s32[1]{0:T(128)} %bitcast.where, s32[56]{0:T(128)} %reshape.22.a_cols, s32[256]{0:T(256)} %reshape.23.p_cols, s32[512]{0:T(512)} %reshape.24.c_cols, bf16[56,128,128]{2,1,0:T(8,128)(2,1)} %bitcast.8, ...), custom_call_target="tpu_custom_call" | custom-call | tf_op jit(solution)/shard_map/pallas_call | solution.py:122
  70.1 0.0 copy-start
  70.1 2.2 %copy-done = f32[4,16,128,128]{3,2,1,0:T(8,128)S(1)} copy-done((f32[4,16,128,128]{3,2,1,0:T(8,128)S(1)}, f32[4,16,128,128]{3,2,1,0:T(8,128)}, u32[]{:S(2)}) %copy-start) | copy-done | bytes 4194328
  72.3 0.0 copy-start.1
  72.3 2.2 %copy-done.1 = s16[2,4,16,128,128]{4,3,2,1,0:T(8,128)(2,1)S(1)} copy-done((s16[2,4,16,128,128]{4,3,2,1,0:T(8,128)(2,1)S(1)}, s16[2,4,16,128,128]{4,3,2,1,0:T(8,128)(2,1)}, u32[]{:S(2)}) %copy-start.1) | copy-done | bytes 4194328
  74.5 0.0 copy-start.2
  74.5 0.8 copy-done.2
  75.3 40.1 %shard_map.56 = f32[16,128,128]{2,1,0:T(8,128)S(1)} custom-call(f32[4,16,128,128]{3,2,1,0:T(8,128)S(1)} %copy-done, s16[2,4,16,128,128]{4,3,2,1,0:T(8,128)(2,1)S(1)} %copy-done.1, f32[2,4,16,128]{3,2,1,0:T(8,128)S(1)} %copy-done.2), custom_call_target="tpu_custom_call" | custom-call | tf_op jit(solution)/shard_map/pallas_call | solution.py:311
  115.4 1.0 copy.15
Async XLA Ops:
  0.0 28.2 %collective-permute-start = (bf16[8,4,128,128]{3,2,1,0:T(8,128)(2,1)}, bf16[8,4,128,128]{3,2,1,0:T(8,128)(2,1)}, u32[]{:S(2)}, u32[]{:S(2)}) collective-permute-start(bf16[8,4,128,128]{3,2,1,0:T(8,128)(2,1)} %param.7), channel_id=1, source_target_pairs={{0,2},{1,3},{2,4},{3,5},{4,6},{5,7},{8,10},{9,11},{10,12},{11,13},... | collective-permute-start | bytes 3145736 | tf_op jit(solution)/shard_map/ppermute | solution.py:17
  3.5 34.9 %collective-permute-start.1 = (bf16[8,4,128,128]{3,2,1,0:T(8,128)(2,1)}, bf16[8,4,128,128]{3,2,1,0:T(8,128)(2,1)}, u32[]{:S(2)}, u32[]{:S(2)}) collective-permute-start(bf16[8,4,128,128]{3,2,1,0:T(8,128)(2,1)} %param.7), channel_id=1, source_target_pairs={{0,1},{1,2},{2,3},{3,4},{4,5},{5,6},{6,7},{8,9},{9,10},{10,11},{11... | collective-permute-start | bytes 3145736 | tf_op jit(solution)/shard_map/ppermute | solution.py:17
  5.4 35.7 %collective-permute-start.2 = (bf16[8,4,128,128]{3,2,1,0:T(8,128)(2,1)}, bf16[8,4,128,128]{3,2,1,0:T(8,128)(2,1)S(1)}, u32[]{:S(2)}, u32[]{:S(2)}) collective-permute-start(bf16[8,4,128,128]{3,2,1,0:T(8,128)(2,1)} %param.7), channel_id=1, source_target_pairs={{1,0},{2,1},{3,2},{4,3},{5,4},{6,5},{7,6},{9,8},{10,9},{11,10},{12... | collective-permute-start | bytes 3145736 | tf_op jit(solution)/shard_map/ppermute | solution.py:17
  9.1 37.0 %collective-permute-start.3 = (bf16[8,4,128,128]{3,2,1,0:T(8,128)(2,1)}, bf16[8,4,128,128]{3,2,1,0:T(8,128)(2,1)S(1)}, u32[]{:S(2)}, u32[]{:S(2)}) collective-permute-start(bf16[8,4,128,128]{3,2,1,0:T(8,128)(2,1)} %param.7), channel_id=1, source_target_pairs={{2,0},{3,1},{4,2},{5,3},{6,4},{7,5},{10,8},{11,9},{12,10},{13,11},... | collective-permute-start | bytes 3145736 | tf_op jit(solution)/shard_map/ppermute | solution.py:17
  46.3 2.3 %copy-start.3 = (bf16[40,4,128,128]{3,2,1,0:T(8,128)(2,1)}, bf16[40,4,128,128]{3,2,1,0:T(8,128)(2,1)S(1)}, u32[]{:S(2)}) copy-start(bf16[40,4,128,128]{3,2,1,0:T(8,128)(2,1)S(1)} %constant_dynamic-update-slice_fusion) | copy-start | bytes 15728644
  70.1 2.2 %copy-start = (f32[4,16,128,128]{3,2,1,0:T(8,128)S(1)}, f32[4,16,128,128]{3,2,1,0:T(8,128)}, u32[]{:S(2)}) copy-start(f32[4,16,128,128]{3,2,1,0:T(8,128)} %get-tuple-element.8.center) | copy-start | bytes 12582916
  72.3 2.2 %copy-start.1 = (s16[2,4,16,128,128]{4,3,2,1,0:T(8,128)(2,1)S(1)}, s16[2,4,16,128,128]{4,3,2,1,0:T(8,128)(2,1)}, u32[]{:S(2)}) copy-start(s16[2,4,16,128,128]{4,3,2,1,0:T(8,128)(2,1)} %get-tuple-element.9.codes) | copy-start | bytes 12582916
  74.5 0.8 copy-start.2

commit v3 on v2

--- a/solution.py
+++ b/solution.py
@@ -9,12 +9,6 @@
 
 RATIO = 2
 REACH = 2
-
-
-def passed_along(x, axis, by):
-    size = lax.axis_size(axis)
-    pairs = [(i, i + by) for i in range(size) if 0 <= i + by < size]
-    return lax.ppermute(x, axis, pairs)
 
 
 LEVELS = 32767.0
@@ -331,6 +325,113 @@
     )(center, codes, scales)
 
 
+def gather_kernel(rows, pieces, own, band, up_sems, down_sems, pair_sems, pass_sems, own_sem):
+    r = lax.axis_index("row")
+    odd = lax.rem(r, 2)
+    partner = r + 1 - 2 * odd
+    has_down = r >= 2
+    has_up = r < rows - 2
+    step = own.shape[0] // pieces
+    barrier = pltpu.get_barrier_semaphore()
+    mesh_type = pl.DeviceIdType.MESH
+
+    def copy(src, dst, sems, c, to):
+        return pltpu.make_async_remote_copy(
+            src_ref=src,
+            dst_ref=dst,
+            send_sem=sems.at[0, c],
+            recv_sem=sems.at[1, c],
+            device_id={"row": to},
+            device_id_type=mesh_type,
+        )
+
+    def part(c):
+        return pl.ds(c * step, step)
+
+    def up(c):
+        return copy(own.at[part(c)], band.at[0, part(c)], up_sems, c, r + 2)
+
+    def down(c):
+        return copy(own.at[part(c)], band.at[4, part(c)], down_sems, c, r - 2)
+
+    def pair():
+        return copy(own, band.at[1 + 2 * odd], pair_sems, 0, partner)
+
+    def passed(c):
+        return copy(
+            band.at[4 - 4 * odd, part(c)], band.at[3 - 2 * odd, part(c)], pass_sems, c, partner
+        )
+
+    def signal(to):
+        pl.semaphore_signal(barrier, inc=1, device_id={"row": to}, device_id_type=mesh_type)
+
+    signal(partner)
+    pl.when(has_up)(lambda: signal(r + 2))
+    pl.when(has_down)(lambda: signal(r - 2))
+    pl.when(has_up & has_down)(lambda: pl.semaphore_wait(barrier, 3))
+    pl.when(jnp.logical_not(has_up & has_down))(lambda: pl.semaphore_wait(barrier, 2))
+
+    for c in range(pieces):
+        pl.when(has_up)(lambda: up(c).start())
+        pl.when(has_down)(lambda: down(c).start())
+    pair().start()
+    local = pltpu.make_async_copy(own, band.at[2], own_sem)
+    local.start()
+
+    @pl.when((odd == 0) & has_up)
+    def _():
+        for c in range(pieces):
+            down(c).wait_recv()
+            passed(c).start()
+
+    @pl.when((odd == 1) & has_down)
+    def _():
+        for c in range(pieces):
+            up(c).wait_recv()
+            passed(c).start()
+
+    @pl.when((odd == 0) & has_down)
+    def _():
+        for c in range(pieces):
+            up(c).wait_recv()
+            passed(c).wait_recv()
+
+    @pl.when((odd == 1) & has_up)
+    def _():
+        for c in range(pieces):
+            down(c).wait_recv()
+            passed(c).wait_recv()
+
+    local.wait()
+    pair().wait_recv()
+    pair().wait_send()
+    for c in range(pieces):
+        pl.when(has_up)(lambda: up(c).wait_send())
+        pl.when(has_down)(lambda: down(c).wait_send())
+
+    @pl.when(((odd == 0) & has_up) | ((odd == 1) & has_down))
+    def _():
+        for c in range(pieces):
+            passed(c).wait_send()
+
+
+def gathered(p_tiles, rows):
+    fine_rows = p_tiles.shape[0]
+    pieces = min(8, fine_rows)
+    vmem = pl.BlockSpec(memory_space=pltpu.VMEM)
+    dma = pltpu.SemaphoreType.DMA
+    return pl.pallas_call(
+        functools.partial(gather_kernel, rows, pieces),
+        out_shape=jax.ShapeDtypeStruct((5,) + p_tiles.shape, p_tiles.dtype),
+        in_specs=[vmem],
+        out_specs=vmem,
+        scratch_shapes=[dma((2, pieces))] * 2 + [dma((2, 1)), dma((2, pieces)), dma],
+        compiler_params=pltpu.CompilerParams(
+            collective_id=1, has_side_effects=True, vmem_limit_bytes=16 * 1024 * 1024
+        ),
+    )(p_tiles)
+
+
 def body(a_tiles, a_cols, p_tiles, p_cols, c_cols):
     fine_rows = a_tiles.shape[0]
     coarse_rows = fine_rows // RATIO
@@ -338,8 +439,8 @@
     kc = c_cols.shape[1]
     chunks = lax.axis_size("grp")
     position = lax.axis_index("row")
-    fetched = [passed_along(p_tiles, "row", offset) for offset in (2, 1, -1, -2)]
-    band = jnp.concatenate([fetched[0], fetched[1], p_tiles, fetched[2], fetched[3]], axis=0)
+    band = gathered(p_tiles, lax.axis_size("row"))
+    band = band.reshape((5 * fine_rows,) + p_tiles.shape[1:])
     center, codes, scales = local_products(
         a_tiles, a_cols, band, p_cols, c_cols, position, chunks
     )

time: 117 us -> 106 us (0.906)
  Pallas kernels: 61.6 us -> 90.9 us
  waiting for transfers between devices: 26.5 us -> 0 us
  starting transfers between devices: 11 us -> 0 us
  local copies, waits for them, and re-layouts: 17.2 us -> 13.9 us
    pallas_call x0 -> x1, Pallas kernels: none -> 27.5 us  [gathered(): pl.pallas_call(functools.partial(gather_kernel, rows, pieces), out_shape=...]
    ppermute x4 -> x0, waiting for transfers between devices: 26.5 us -> none  [passed_along(): return lax.ppermute(x, axis, pairs)]
    ppermute x4 -> x0, starting transfers between devices: 11 us -> none  [passed_along(): return lax.ppermute(x, axis, pairs)]
    unnamed x16 -> x14, local copies, waits for them, and re-layouts: 15.1 us -> 12 us
    pallas_call x1, Pallas kernels: 40.1 us -> 41.9 us  [exchange(): pl.pallas_call(functools.partial(exchange_kernel, rows, chunks), out_shap...]
  transfers between devices with their start and end apart: 4 -> 0, of which waited for: 3 -> 0; matrix products, arithmetic and copies ran while one was open for 7% -> 0% of each run, Pallas kernels for 0% -> 0%
where the time goes in v3:
time: 106 us; the launch traced here: 105 us
  Pallas kernels  90.9 us (86%)
  local copies, waits for them, and re-layouts  13.9 us (13%)
    pallas_call x1, Pallas kernels, exchange(): pl.pallas_call(functools.partial(exchange_kernel, rows, chunks), out_shap...  41.9 us
    pallas_call x1, Pallas kernels, gathered(): pl.pallas_call(functools.partial(gather_kernel, rows, pieces), out_shape=...  27.5 us
    pallas_call x1, Pallas kernels, local_products(): pl.pallas_call(functools.partial(product_kernel, (fine_rows, slots, kp, k...  21.6 us
    unnamed x14, local copies, waits for them, and re-layouts  12 us

profile of v3, /device:TPU:10, one launch (start us, length us, event | category | flops | bytes accessed | tf_op | source)
XLA Modules:
  0.0 104.9 jit_solution(16331809371807814281)
XLA Ops:
  0.0 0.8 copy.7
  0.8 0.6 reshape.19.a_cols
  1.4 0.8 copy.9
  2.1 0.7 reshape.21.c_cols
  2.8 0.8 copy.8
  3.6 0.7 reshape.20.p_cols
  4.2 0.0 copy-start.3
  4.2 1.2 %copy-done.3 = bf16[8,4,128,128]{3,2,1,0:T(8,128)(2,1)S(1)} copy-done((bf16[8,4,128,128]{3,2,1,0:T(8,128)(2,1)S(1)}, bf16[8,4,128,128]{3,2,1,0:T(8,128)(2,1)}, u32[]{:S(2)}) %copy-start.3) | copy-done | bytes 1048600
  5.5 27.5 %shard_map.55 = bf16[5,8,4,128,128]{4,3,2,1,0:T(8,128)(2,1)S(1)} custom-call(bf16[8,4,128,128]{3,2,1,0:T(8,128)(2,1)S(1)} %copy-done.3), custom_call_target="tpu_custom_call" | custom-call | tf_op jit(solution)/shard_map/pallas_call | solution.py:423
  32.9 0.0 copy-start
  33.0 2.3 %copy-done = bf16[5,8,4,128,128]{4,3,2,1,0:T(8,128)(2,1)} copy-done((bf16[5,8,4,128,128]{4,3,2,1,0:T(8,128)(2,1)}, bf16[5,8,4,128,128]{4,3,2,1,0:T(8,128)(2,1)S(1)}, u32[]{:S(2)}) %copy-start) | copy-done | bytes 5242904
  35.2 21.6 %shard_map.56 = (f32[4,16,128,128]{3,2,1,0:T(8,128)}, s16[2,4,16,128,128]{4,3,2,1,0:T(8,128)(2,1)}, f32[2,4,16,128]{3,2,1,0:T(8,128)}) custom-call(s32[1]{0:T(128)} %bitcast.where, s32[56]{0:T(128)} %reshape.19.a_cols, s32[256]{0:T(256)} %reshape.20.p_cols, s32[512]{0:T(512)} %reshape.21.c_cols, bf16[56,128,128]{2,1,0:T(8,128)(2,1)} %bitcast.8, ...), custom_call_target="tpu_custom_call" | custom-call | tf_op jit(solution)/shard_map/pallas_call | solution.py:116
  56.8 0.0 copy-start.1
  56.8 2.2 %copy-done.1 = f32[4,16,128,128]{3,2,1,0:T(8,128)S(1)} copy-done((f32[4,16,128,128]{3,2,1,0:T(8,128)S(1)}, f32[4,16,128,128]{3,2,1,0:T(8,128)}, u32[]{:S(2)}) %copy-start.1) | copy-done | bytes 4194328
  59.0 0.0 copy-start.2
  59.0 2.2 %copy-done.2 = s16[2,4,16,128,128]{4,3,2,1,0:T(8,128)(2,1)S(1)} copy-done((s16[2,4,16,128,128]{4,3,2,1,0:T(8,128)(2,1)S(1)}, s16[2,4,16,128,128]{4,3,2,1,0:T(8,128)(2,1)}, u32[]{:S(2)}) %copy-start.2) | copy-done | bytes 4194328
  61.2 0.0 copy-start.4
  61.2 0.8 copy-done.4
  62.0 41.9 %shard_map.57 = f32[16,128,128]{2,1,0:T(8,128)S(1)} custom-call(f32[4,16,128,128]{3,2,1,0:T(8,128)S(1)} %copy-done.1, s16[2,4,16,128,128]{4,3,2,1,0:T(8,128)(2,1)S(1)} %copy-done.2, f32[2,4,16,128]{3,2,1,0:T(8,128)S(1)} %copy-done.4), custom_call_target="tpu_custom_call" | custom-call | tf_op jit(solution)/shard_map/pallas_call | solution.py:305
  103.9 1.0 copy.11
Async XLA Ops:
  4.2 1.2 %copy-start.3 = (bf16[8,4,128,128]{3,2,1,0:T(8,128)(2,1)S(1)}, bf16[8,4,128,128]{3,2,1,0:T(8,128)(2,1)}, u32[]{:S(2)}) copy-start(bf16[8,4,128,128]{3,2,1,0:T(8,128)(2,1)} %own.1) | copy-start | bytes 3145732
  32.9 2.3 %copy-start = (bf16[5,8,4,128,128]{4,3,2,1,0:T(8,128)(2,1)}, bf16[5,8,4,128,128]{4,3,2,1,0:T(8,128)(2,1)S(1)}, u32[]{:S(2)}) copy-start(bf16[5,8,4,128,128]{4,3,2,1,0:T(8,128)(2,1)S(1)} %shard_map.55) | copy-start | bytes 15728644
  56.8 2.2 %copy-start.1 = (f32[4,16,128,128]{3,2,1,0:T(8,128)S(1)}, f32[4,16,128,128]{3,2,1,0:T(8,128)}, u32[]{:S(2)}) copy-start(f32[4,16,128,128]{3,2,1,0:T(8,128)} %get-tuple-element.8.center) | copy-start | bytes 12582916
  59.0 2.2 %copy-start.2 = (s16[2,4,16,128,128]{4,3,2,1,0:T(8,128)(2,1)S(1)}, s16[2,4,16,128,128]{4,3,2,1,0:T(8,128)(2,1)}, u32[]{:S(2)}) copy-start(s16[2,4,16,128,128]{4,3,2,1,0:T(8,128)(2,1)} %get-tuple-element.9.codes) | copy-start | bytes 12582916
  61.2 0.8 copy-start.4
